TPU v7x, 32 devices: a whole 2x2x4 slice. The times are simulated.
32 devices in a mesh: gx: 2 (over x), gy: 4 (over y, core), gz: 4 (over z).
Axes of the slice: x: 2, y: 2, z: 4, core: 2. Of those that a mesh axis runs over, the one named last changes fastest.
Arguments:
- images: bfloat16 [32, 5, 524288], P(('gx', 'gy', 'gz')), may hold values from 0 to 0.125
- order: int32 [32], replicated, may hold values from 0 to 31, as said below
Outputs:
- frame: float32 [5, 524288], P(None, 'gx')
Inputs may be any that keep to these rules, and one draw needn't show every extreme that they name: order is a permutation of the bricks, where brick r sits at index r // 16 along gx, (r // 4) % 4 along gy and r % 4 along gz; the bricks of one gz index take consecutive places, within them the bricks of one (gy, gz) pair take consecutive places; the order of gz indices, the order of gy indices within each gz index and the order of gx indices within each (gy, gz) pair are arbitrary and may differ from slab to slab and from column to column.
All inputs are finite; a program needn't handle non-finite values.
Results may differ from a plain program's by a relative error of at most 0.0003.
Values may be sent and summed in bfloat16 or wider, within the bound.
A program may use at most 64 MiB of HBM per device.

v0:
```python
import jax
import jax.numpy as jnp
from jax import lax
from jax.sharding import PartitionSpec as P


def composite(stacked, member_keys):
    ranked = jnp.argsort(member_keys)

    def layer(total, member):
        picture = lax.dynamic_index_in_dim(stacked, member, 0, keepdims=False).astype(jnp.float32)
        return (total + (1.0 - total[4:5]) * picture, None)

    start = jnp.zeros(stacked.shape[1:], jnp.float32)
    total, _ = lax.scan(layer, start, ranked)
    return total[None]


def per_device(images, order):
    count_x = lax.axis_size("gx")
    count_y = lax.axis_size("gy")
    count_z = lax.axis_size("gz")
    bricks_all = count_x * count_y * count_z
    place_z = lax.axis_index("gz")
    grid_order = order.reshape(count_x, count_y, count_z)
    column_order = lax.dynamic_index_in_dim(grid_order, place_z, 2, keepdims=False)
    pixels = images.shape[2]
    layers = images.reshape(1, images.shape[1], bricks_all, pixels // bricks_all)
    joined_keys = column_order.reshape(-1)
    partial_value = composite(
        lax.all_to_all(layers, ("gx", "gy"), split_axis=2, concat_axis=0, tiled=True), joined_keys
    )
    slab_keys = jnp.min(grid_order, axis=(0, 1))
    partial_value = composite(
        lax.all_to_all(partial_value, "gz", split_axis=2, concat_axis=0, tiled=True), slab_keys
    )
    tiles = lax.all_gather(partial_value, ("gy", "gz"), axis=2, tiled=True)
    return tiles.reshape(tiles.shape[1], -1)


def solution(mesh):
    in_specs = (P(("gx", "gy", "gz"), None, None), P())
    out_specs = P(None, "gx")
    return jax.shard_map(
        per_device, mesh=mesh, in_specs=in_specs, out_specs=out_specs, check_vma=False
    )
```

profile of v0, /device:TPU:0, one launch (start us, length us, event | category | flops | bytes accessed | tf_op | source)
XLA Modules:
  0.0 295.9 jit_solution(15883542343164375677)
XLA Ops:
  6.5 5.3 %all-to-all-start = ((bf16[1,5,32,16384]{3,1,0,2:T(8,128)(2,1)}), bf16[1,5,32,16384]{3,1,0,2:T(8,128)(2,1)}, u32[]{:S(2)}, u32[]{:S(2)}) async-start(bf16[1,5,32,16384]{3,1,0,2:T(8,128)(2,1)} %bitcast.44), calls=%async_computation | async-start | bytes 16777216 | tf_op jit(solution)/shard_map/all_to_all | solution.py:31
  12.3 1.0 sort.35
  13.2 92.2 %all-to-all-done = bf16[1,5,32,16384]{3,1,0,2:T(8,128)(2,1)} async-done(((bf16[1,5,32,16384]{3,1,0,2:T(8,128)(2,1)}), bf16[1,5,32,16384]{3,1,0,2:T(8,128)(2,1)}, u32[]{:S(2)}, u32[]{:S(2)}) %all-to-all-start) | async-done | bytes 5242912 | tf_op jit(solution)/shard_map/all_to_all | solution.py:31
  105.4 10.4 %copy.29 = bf16[1,5,8,4,16384]{4,3,1,2,0:T(4,128)(2,1)} copy(bf16[1,5,8,4,16384]{4,1,3,2,0:T(8,128)(2,1)} %bitcast.1) | data formatting | bytes 10485760 | tf_op jit(solution)/shard_map/all_to_all | solution.py:31
  115.8 39.8 %while.22 = (s32[]{:T(128)}, f32[5,4,16384]{2,1,0:T(4,128)S(1)}, s32[8]{0:T(128)S(1)}, bf16[8,5,4,16384]{3,2,1,0:T(4,128)(2,1)}, s32[]{:T(128)}, /*index=5*/s32[]{:T(128)}, s32[]{:T(128)}) while((s32[]{:T(128)}, f32[5,4,16384]{2,1,0:T(4,128)S(1)}, s32[8]{0:T(128)S(1)}, bf16[8,5,4,16384]{3,2,1,0:T(4,128)(2,1)}, s32[]{:T(128)}, ...), condition=%wide.region_4.5_spmd.clone, body=%wide.region_3.4_spmd.clone.sunk | while | flops 1703942 | bytes 6684818 | solution.py:15
  115.8 0.7 dynamic_slice.33
  118.6 0.3 broadcast_select_fusion.4
  118.9 1.8 fusion.7
  120.8 0.7 dynamic_slice.33
  123.5 0.3 broadcast_select_fusion.4
  123.9 1.8 fusion.7
  125.8 0.7 dynamic_slice.33
  128.5 0.3 broadcast_select_fusion.4
  128.9 1.8 fusion.7
  130.7 0.7 dynamic_slice.33
  133.5 0.3 broadcast_select_fusion.4
  133.9 1.8 fusion.7
  135.7 0.7 dynamic_slice.33
  138.5 0.3 broadcast_select_fusion.4
  138.8 1.8 fusion.7
  140.7 0.7 dynamic_slice.33
  143.4 0.3 broadcast_select_fusion.4
  143.8 1.8 fusion.7
  145.7 0.7 dynamic_slice.33
  148.4 0.3 broadcast_select_fusion.4
  148.8 1.8 fusion.7
  150.6 0.7 dynamic_slice.33
  153.4 0.3 broadcast_select_fusion.4
  153.8 1.8 fusion.7
  155.6 2.4 copy.20
  158.0 5.7 %all-to-all-start.1 = ((f32[1,5,4,16384]{3,0,1,2:T(1,128)}), f32[1,5,4,16384]{3,0,1,2:T(1,128)S(1)}, u32[]{:S(2)}, u32[]{:S(2)}) async-start(f32[1,5,4,16384]{3,0,1,2:T(1,128)} %copy.20), calls=%async_computation.1 | async-start | bytes 2621440 | tf_op jit(solution)/shard_map/all_to_all | solution.py:35
  163.7 0.7 sort.34
  164.5 30.3 %all-to-all-done.1 = f32[1,5,4,16384]{3,0,1,2:T(1,128)S(1)} async-done(((f32[1,5,4,16384]{3,0,1,2:T(1,128)}), f32[1,5,4,16384]{3,0,1,2:T(1,128)S(1)}, u32[]{:S(2)}, u32[]{:S(2)}) %all-to-all-start.1) | async-done | bytes 1310752 | tf_op jit(solution)/shard_map/all_to_all | solution.py:35
  194.7 0.8 copy.30
  195.6 14.0 %while.23 = (s32[]{:T(128)}, f32[5,1,16384]{2,1,0:T(1,128)S(1)}, s32[4]{0:T(128)S(1)}, f32[4,5,1,16384]{3,0,1,2:T(4,128)S(1)}, s32[]{:T(128)}, /*index=5*/s32[]{:T(128)}, s32[]{:T(128)}) while((s32[]{:T(128)}, f32[5,1,16384]{2,1,0:T(1,128)S(1)}, s32[4]{0:T(128)S(1)}, f32[4,5,1,16384]{3,0,1,2:T(4,128)S(1)}, s32[]{:T(128)}, ...), condition=%wide.region_6.7_spmd.clone, body=%wide.region_5.6_spmd.clone.sunk | while | flops 344070 | bytes 1835154 | solution.py:15
  195.6 0.6 dynamic_slice.35
  198.1 0.3 broadcast_select_fusion.5
  198.5 0.6 fusion.8
  199.1 0.6 dynamic_slice.35
  201.6 0.3 broadcast_select_fusion.5
  202.0 0.6 fusion.8
  202.6 0.6 dynamic_slice.35
  205.5 0.6 fusion.8
  206.1 0.6 dynamic_slice.35
  209.0 0.6 fusion.8
  209.6 1.0 copy.23
  210.7 72.6 %all-gather.3.cloned.1.call-done = f32[5,16,16384]{2,0,1:T(8,128)} async-done(((f32[5,1,16384]{2,0,1:T(8,128)}), f32[5,16,16384]{2,0,1:T(8,128)}) %all-gather.3.cloned.1.call-update) | async-done | bytes 5242896 | tf_op jit(solution)/shard_map/all_gather | solution.py:37
  283.2 5.9 %copy.44 = f32[5,262144]{1,0:T(8,128)} copy(f32[5,262144]{1,0:T(8,128)} %bitcast.45) | data formatting | bytes 10485760
  (26 shorter events, 1.7 us)
Async XLA Ops:
  6.5 5.3 %copy-start = (s32[32]{0:T(128)S(1)}, s32[32]{0:T(128)}, u32[]{:S(2)}) copy-start(s32[32]{0:T(128)} %param.7) | copy-start | bytes 388
  6.5 98.9 %all-to-all-start = ((bf16[1,5,32,16384]{3,1,0,2:T(8,128)(2,1)}), bf16[1,5,32,16384]{3,1,0,2:T(8,128)(2,1)}, u32[]{:S(2)}, u32[]{:S(2)}) async-start(bf16[1,5,32,16384]{3,1,0,2:T(8,128)(2,1)} %bitcast.44), calls=%async_computation | async-start | bytes 16777216 | tf_op jit(solution)/shard_map/all_to_all | solution.py:31
  158.0 36.7 %all-to-all-start.1 = ((f32[1,5,4,16384]{3,0,1,2:T(1,128)}), f32[1,5,4,16384]{3,0,1,2:T(1,128)S(1)}, u32[]{:S(2)}, u32[]{:S(2)}) async-start(f32[1,5,4,16384]{3,0,1,2:T(1,128)} %copy.20), calls=%async_computation.1 | async-start | bytes 2621440 | tf_op jit(solution)/shard_map/all_to_all | solution.py:35
  163.7 119.6 %all-gather.3.cloned.1.call-start = ((), (), s32[]{:S(2)}) async-start(), calls=%async_computation.2 | async-start | bytes 8912896 | tf_op jit(solution)/shard_map/all_gather | solution.py:37
Sparse Core Ops, SparseCore 0:
  210.8 72.4 all-gather.2
where the time goes:
time: 297 us; the launch traced here: 296 us
  waiting for transfers between devices  195 us (66%)
  local copies, waits for them, and re-layouts  28.6 us (10%)
  loops' own time  24.8 us (8%)
  other arithmetic  23.1 us (8%)
  between operations  13.4 us (5%)
  starting transfers between devices  11 us (4%)
    all_to_all x1, waiting for transfers between devices, per_device(): lax.all_to_all(layers, ('gx', 'gy'), split_axis=2, concat_axis=0, tiled=T...  92.2 us
    all_gather x1, waiting for transfers between devices, per_device(): tiles = lax.all_gather(partial_value, ('gy', 'gz'), axis=2, tiled=True)  72.6 us
    all_to_all x1, waiting for transfers between devices, per_device(): lax.all_to_all(partial_value, 'gz', split_axis=2, concat_axis=0, tiled=True)  30.3 us
    another operation x2, loops' own time, composite(): total, _ = lax.scan(layer, start, ranked)  24.8 us
    add x12, other arithmetic, layer(): return (total + (1.0 - total[4:5]) * picture, None)  17 us
    all_to_all x1, local copies, waits for them, and re-layouts, per_device(): lax.all_to_all(layers, ('gx', 'gy'), split_axis=2, concat_axis=0, tiled=T...  10.4 us
    dynamic_slice x12, local copies, waits for them, and re-layouts, composite(): total, _ = lax.scan(layer, start, ranked)  7.7 us
  transfers between devices with their start and end apart: 3, of which 3 were waited for; matrix products, arithmetic and copies ran while one was open for 1% of the time, Pallas kernels for 0%

commit v1 on v0

--- a/solution.py
+++ b/solution.py
@@ -34,7 +34,7 @@
     partial_value = composite(
         lax.all_to_all(partial_value, "gz", split_axis=2, concat_axis=0, tiled=True), slab_keys
     )
-    tiles = lax.all_gather(partial_value, ("gy", "gz"), axis=2, tiled=True)
+    tiles = jnp.concatenate(lax.all_gather(partial_value, ("gy", "gz")), axis=2)
     return tiles.reshape(tiles.shape[1], -1)
 
 

time: 297 us -> 285 us (0.960)
  waiting for transfers between devices: 195 us -> 177 us
  local copies, waits for them, and re-layouts: 28.6 us -> 34.8 us
    all_gather x1, waiting for transfers between devices: 72.6 us -> 54 us  [per_device(): tiles = jnp.concatenate(lax.all_gather(partial_value, ('gy', 'gz')), axis=2)]
    reshape x0 -> x1, local copies, waits for them, and re-layouts: none -> 5.74 us  [per_device(): tiles = jnp.concatenate(lax.all_gather(partial_value, ('gy', 'gz')), axis=2)]
    unnamed x3 -> x5, local copies, waits for them, and re-layouts: 5.85 us -> 7.36 us
where the time goes in v1:
time: 285 us; the launch traced here: 284 us
  waiting for transfers between devices  177 us (62%)
  local copies, waits for them, and re-layouts  34.8 us (12%)
  loops' own time  24.8 us (9%)
  other arithmetic  23.1 us (8%)
  between operations  13.4 us (5%)
  starting transfers between devices  11 us (4%)
    all_to_all x1, waiting for transfers between devices, per_device(): lax.all_to_all(layers, ('gx', 'gy'), split_axis=2, concat_axis=0, tiled=T...  92.2 us
    all_gather x1, waiting for transfers between devices, per_device(): tiles = jnp.concatenate(lax.all_gather(partial_value, ('gy', 'gz')), axis=2)  54 us
    all_to_all x1, waiting for transfers between devices, per_device(): lax.all_to_all(partial_value, 'gz', split_axis=2, concat_axis=0, tiled=True)  30.3 us
    another operation x2, loops' own time, composite(): total, _ = lax.scan(layer, start, ranked)  24.8 us
    add x12, other arithmetic, layer(): return (total + (1.0 - total[4:5]) * picture, None)  17 us
    all_to_all x1, local copies, waits for them, and re-layouts, per_device(): lax.all_to_all(layers, ('gx', 'gy'), split_axis=2, concat_axis=0, tiled=T...  10.4 us
    dynamic_slice x12, local copies, waits for them, and re-layouts, composite(): total, _ = lax.scan(layer, start, ranked)  7.7 us
    unnamed x5, local copies, waits for them, and re-layouts  7.36 us
  transfers between devices with their start and end apart: 3, of which 3 were waited for; matrix products, arithmetic and copies ran while one was open for 1% of the time, Pallas kernels for 0%

profile of v1, /device:TPU:0, one launch (start us, length us, event | category | flops | bytes accessed | tf_op | source)
XLA Modules:
  0.0 283.6 jit_solution(13748867691269585028)
XLA Ops:
  6.5 5.3 %all-to-all-start = ((bf16[1,5,32,16384]{3,1,0,2:T(8,128)(2,1)}), bf16[1,5,32,16384]{3,1,0,2:T(8,128)(2,1)}, u32[]{:S(2)}, u32[]{:S(2)}) async-start(bf16[1,5,32,16384]{3,1,0,2:T(8,128)(2,1)} %bitcast.53), calls=%async_computation | async-start | bytes 16777216 | tf_op jit(solution)/shard_map/all_to_all | solution.py:31
  12.3 1.0 sort.35
  13.2 92.2 %all-to-all-done = bf16[1,5,32,16384]{3,1,0,2:T(8,128)(2,1)} async-done(((bf16[1,5,32,16384]{3,1,0,2:T(8,128)(2,1)}), bf16[1,5,32,16384]{3,1,0,2:T(8,128)(2,1)}, u32[]{:S(2)}, u32[]{:S(2)}) %all-to-all-start) | async-done | bytes 5242912 | tf_op jit(solution)/shard_map/all_to_all | solution.py:31
  105.4 10.4 %copy.33 = bf16[1,5,8,4,16384]{4,3,1,2,0:T(4,128)(2,1)} copy(bf16[1,5,8,4,16384]{4,1,3,2,0:T(8,128)(2,1)} %bitcast.1) | data formatting | bytes 10485760 | tf_op jit(solution)/shard_map/all_to_all | solution.py:31
  115.8 39.8 %while.22 = (s32[]{:T(128)}, f32[5,4,16384]{2,1,0:T(4,128)S(1)}, s32[8]{0:T(128)S(1)}, bf16[8,5,4,16384]{3,2,1,0:T(4,128)(2,1)}, s32[]{:T(128)}, /*index=5*/s32[]{:T(128)}, s32[]{:T(128)}) while((s32[]{:T(128)}, f32[5,4,16384]{2,1,0:T(4,128)S(1)}, s32[8]{0:T(128)S(1)}, bf16[8,5,4,16384]{3,2,1,0:T(4,128)(2,1)}, s32[]{:T(128)}, ...), condition=%wide.region_4.5_spmd.clone, body=%wide.region_3.4_spmd.clone.sunk | while | flops 1703942 | bytes 6684818 | solution.py:15
  115.8 0.7 dynamic_slice.33
  118.6 0.3 broadcast_select_fusion.4
  118.9 1.8 fusion.7
  120.8 0.7 dynamic_slice.33
  123.5 0.3 broadcast_select_fusion.4
  123.9 1.8 fusion.7
  125.8 0.7 dynamic_slice.33
  128.5 0.3 broadcast_select_fusion.4
  128.9 1.8 fusion.7
  130.7 0.7 dynamic_slice.33
  133.5 0.3 broadcast_select_fusion.4
  133.9 1.8 fusion.7
  135.7 0.7 dynamic_slice.33
  138.8 1.8 fusion.7
  140.7 0.7 dynamic_slice.33
  143.8 1.8 fusion.7
  145.7 0.7 dynamic_slice.33
  148.4 0.3 broadcast_select_fusion.4
  148.8 1.8 fusion.7
  150.6 0.7 dynamic_slice.33
  153.4 0.3 broadcast_select_fusion.4
  153.8 1.8 fusion.7
  155.6 2.4 copy.22
  158.0 5.7 %all-to-all-start.1 = ((f32[1,5,4,16384]{3,0,1,2:T(1,128)}), f32[1,5,4,16384]{3,0,1,2:T(1,128)S(1)}, u32[]{:S(2)}, u32[]{:S(2)}) async-start(f32[1,5,4,16384]{3,0,1,2:T(1,128)} %copy.22), calls=%async_computation.1 | async-start | bytes 2621440 | tf_op jit(solution)/shard_map/all_to_all | solution.py:35
  163.7 0.7 sort.34
  164.5 30.3 %all-to-all-done.1 = f32[1,5,4,16384]{3,0,1,2:T(1,128)S(1)} async-done(((f32[1,5,4,16384]{3,0,1,2:T(1,128)}), f32[1,5,4,16384]{3,0,1,2:T(1,128)S(1)}, u32[]{:S(2)}, u32[]{:S(2)}) %all-to-all-start.1) | async-done | bytes 1310752 | tf_op jit(solution)/shard_map/all_to_all | solution.py:35
  194.7 0.8 copy.35
  195.6 14.0 %while.23 = (s32[]{:T(128)}, f32[5,1,16384]{2,1,0:T(1,128)S(1)}, s32[4]{0:T(128)S(1)}, f32[4,5,1,16384]{3,0,1,2:T(4,128)S(1)}, s32[]{:T(128)}, /*index=5*/s32[]{:T(128)}, s32[]{:T(128)}) while((s32[]{:T(128)}, f32[5,1,16384]{2,1,0:T(1,128)S(1)}, s32[4]{0:T(128)S(1)}, f32[4,5,1,16384]{3,0,1,2:T(4,128)S(1)}, s32[]{:T(128)}, ...), condition=%wide.region_6.7_spmd.clone, body=%wide.region_5.6_spmd.clone.sunk | while | flops 344070 | bytes 1835154 | solution.py:15
  195.6 0.6 dynamic_slice.35
  198.1 0.3 broadcast_select_fusion.5
  198.5 0.6 fusion.8
  199.1 0.6 dynamic_slice.35
  201.6 0.3 broadcast_select_fusion.5
  202.0 0.6 fusion.8
  202.6 0.6 dynamic_slice.35
  205.5 0.6 fusion.8
  206.1 0.6 dynamic_slice.35
  208.7 0.3 broadcast_select_fusion.5
  209.0 0.6 fusion.8
  209.6 0.7 copy-done
  210.4 54.0 %all-gather.3.cloned.1.call-done = f32[80,1,16384]{2,1,0:T(1,128)} async-done(((f32[5,1,16384]{2,1,0:T(1,128)}), f32[80,1,16384]{2,1,0:T(1,128)}) %all-gather.3.cloned.1.call-update) | async-done | bytes 5242896 | tf_op jit(solution)/shard_map/all_gather | solution.py:37
  264.4 5.7 %copy.34 = f32[1,5,16,1,16384]{4,2,1,3,0:T(8,128)S(1)} copy(f32[1,5,16,1,16384]{4,3,1,0,2:T(1,128)} %bitcast.56) | data formatting | bytes 10485760 | tf_op jit(solution)/shard_map/reshape | solution.py:37
  270.1 6.6 %copy.29 = f32[1,5,16,16384]{3,1,2,0:T(8,128)} copy(f32[1,5,16,16384]{3,2,1,0:T(8,128)S(1)} %bitcast.51) | data formatting | bytes 10485760
  (28 shorter events, 2.1 us)
Async XLA Ops:
  6.5 5.3 %copy-start.1 = (s32[32]{0:T(128)S(1)}, s32[32]{0:T(128)}, u32[]{:S(2)}) copy-start(s32[32]{0:T(128)} %param.7) | copy-start | bytes 388
  6.5 98.9 %all-to-all-start = ((bf16[1,5,32,16384]{3,1,0,2:T(8,128)(2,1)}), bf16[1,5,32,16384]{3,1,0,2:T(8,128)(2,1)}, u32[]{:S(2)}, u32[]{:S(2)}) async-start(bf16[1,5,32,16384]{3,1,0,2:T(8,128)(2,1)} %bitcast.53), calls=%async_computation | async-start | bytes 16777216 | tf_op jit(solution)/shard_map/all_to_all | solution.py:31
  158.0 36.7 %all-to-all-start.1 = ((f32[1,5,4,16384]{3,0,1,2:T(1,128)}), f32[1,5,4,16384]{3,0,1,2:T(1,128)S(1)}, u32[]{:S(2)}, u32[]{:S(2)}) async-start(f32[1,5,4,16384]{3,0,1,2:T(1,128)} %copy.22), calls=%async_computation.1 | async-start | bytes 2621440 | tf_op jit(solution)/shard_map/all_to_all | solution.py:35
  163.7 100.7 %all-gather.3.cloned.1.call-start = ((), (), s32[]{:S(2)}) async-start(), calls=%async_computation.2 | async-start | bytes 5570560 | tf_op jit(solution)/shard_map/all_gather | solution.py:37
  209.6 0.7 copy-start
Sparse Core Ops, SparseCore 0:
  210.5 53.8 all-gather.2
